TPU v7x, 32 devices: a whole 2x2x4 slice. The times are simulated.
32 devices in a mesh: par: 4 (over x, core), freq: 8 (over z, y).
Axes of the slice: x: 2, y: 2, z: 4, core: 2. Of those that a mesh axis runs over, the one named last changes fastest.
Arguments:
- probes: bfloat16 [64, 600, 420], P('freq'), may hold values from -6 to 6
- map_real: bfloat16 [112, 600, 1024], P('freq', None, 'par'), may hold values from -0.1875 to 0.1875
- map_imag: bfloat16 [112, 600, 1024], P('freq', None, 'par'), may hold values from -0.1875 to 0.1875
- prior_var: float32 [1024], P('par'), may hold values from 0.05 to 13, as said below
Outputs:
- applied: bfloat16 [64, 600, 420], P('freq')
Inputs may be any that keep to these rules, and one draw needn't show every extreme that they name: `prior_var`: prior variances are positive.
All inputs are finite; a program needn't handle non-finite values.
Results may differ from a plain program's by a relative error of at most 0.014.
Values may be sent and summed in bfloat16 or wider, within the bound.
A program may use at most 64 MiB of HBM per device.

v0:
```python
import jax
import jax.numpy as jnp
from jax import lax
from jax.sharding import PartitionSpec as P

SENSORS = 600
STEPS = 420
PERIOD = 840
PROBES = 64


noise_ratio = 0.5


def split_product(left, table):
    upper = table.astype(jnp.bfloat16)
    lower = (table - upper.astype(jnp.float32)).astype(jnp.bfloat16)
    return jnp.dot(left, upper, preferred_element_type=jnp.float32) + jnp.dot(
        left, lower, preferred_element_type=jnp.float32
    )


def shards(probes, map_real, map_imag, prior_var):
    freq_count = lax.axis_size("freq")
    bins_dev = map_real.shape[0]
    probe_block = probes.shape[0]
    total_bins = bins_dev * freq_count
    time_steps = jnp.arange(STEPS, dtype=jnp.int32)
    bin_index = jnp.arange(total_bins, dtype=jnp.int32)
    product_index = time_steps[:, None] * bin_index[None, :] % PERIOD
    angles = product_index.astype(jnp.float32) * (2.0 * jnp.pi / PERIOD)
    norm_scale = 1.0 / jnp.sqrt(jnp.float32(PERIOD))
    cosines = jnp.cos(angles) * norm_scale
    sines = jnp.sin(angles) * norm_scale
    forward = jnp.stack([cosines, -sines], axis=2).reshape(STEPS, 2 * total_bins)
    all_weight = jnp.where(bin_index == 0, 1.0, 2.0).astype(jnp.float32)
    inverse = jnp.stack([cosines * all_weight[None, :], -sines * all_weight[None, :]], axis=2)
    inverse = inverse.reshape(STEPS, 2 * total_bins).T
    flattened = probes.reshape(probe_block * SENSORS, STEPS)
    spectrum = split_product(flattened, forward).astype(jnp.bfloat16)
    spectrum = spectrum.reshape(probe_block, SENSORS, 2 * total_bins)
    exchanged = lax.all_to_all(spectrum, "freq", split_axis=2, concat_axis=0, tiled=True)
    all_probes = exchanged.shape[0]
    operand = exchanged.reshape(all_probes, SENSORS, bins_dev, 2).transpose(2, 1, 3, 0)
    operand = operand.reshape(bins_dev, SENSORS, 2 * all_probes)
    left_real = jnp.einsum("ksp,ksc->kpc", map_real, operand, preferred_element_type=jnp.float32)
    left_imag = jnp.einsum("ksp,ksc->kpc", map_imag, operand, preferred_element_type=jnp.float32)
    u_real = left_real[..., :all_probes] + left_imag[..., all_probes:]
    u_imag = left_real[..., all_probes:] - left_imag[..., :all_probes]
    global_bin = lax.axis_index("freq") * bins_dev + jnp.arange(bins_dev, dtype=jnp.int32)
    bin_weight = jnp.where(global_bin == 0, 1.0, 2.0).astype(jnp.float32)
    quadratic = jnp.sum(
        bin_weight[:, None, None] * prior_var[None, :, None] * (u_real * u_real + u_imag * u_imag)
    )
    trace_est = lax.psum(quadratic, ("par", "freq")) / (PROBES * SENSORS * STEPS)
    scaled = (jnp.concatenate([u_real, u_imag], axis=-1) * prior_var[None, :, None]).astype(
        jnp.bfloat16
    )
    right_real = jnp.einsum("ksp,kpc->ksc", map_real, scaled, preferred_element_type=jnp.float32)
    right_imag = jnp.einsum("ksp,kpc->ksc", map_imag, scaled, preferred_element_type=jnp.float32)
    w_partial = jnp.concatenate(
        [
            right_real[..., :all_probes] - right_imag[..., all_probes:],
            right_real[..., all_probes:] + right_imag[..., :all_probes],
        ],
        axis=-1,
    )
    summed = lax.psum(w_partial.astype(jnp.bfloat16), "par")
    outgoing = summed.reshape(bins_dev, SENSORS, 2, all_probes).transpose(3, 1, 0, 2)
    outgoing = outgoing.reshape(all_probes, SENSORS, 2 * bins_dev)
    by_probe = lax.all_to_all(outgoing, "freq", split_axis=0, concat_axis=2, tiled=True)
    by_rows = by_probe.reshape(probe_block * SENSORS, 2 * total_bins)
    response = split_product(by_rows, inverse).reshape(probe_block, SENSORS, STEPS)
    return (response + noise_ratio * trace_est * probes.astype(jnp.float32)).astype(jnp.bfloat16)


def solution(mesh):
    placed = (P("freq", None, None), P("freq", None, "par"), P("freq", None, "par"), P("par"))
    return jax.shard_map(
        shards, mesh=mesh, in_specs=placed, out_specs=P("freq", None, None), check_vma=False
    )
```

profile of v0, /device:TPU:0, one launch (start us, length us, event | category | flops | bytes accessed | tf_op | source)
XLA Modules:
  0.0 288.2 jit_solution(12911080688204210552)
XLA Ops:
  6.5 7.8 %multiply_negate_fusion = (f32[420,112,1]{0,2,1:T(1,128)S(1)}, f32[420,112,1]{0,2,1:T(1,128)S(1)}) fusion(), kind=kLoop, calls=%fused_computation.29 | loop fusion | flops 564480 | bytes 376320 | tf_op jit(solution)/shard_map/neg | solution.py:35
  14.4 0.5 subtract_convert_fusion
  14.8 0.4 fusion.9
  15.7 8.0 %reshape.201 = bf16[4800,420]{0,1:T(8,128)(2,1)} reshape(bf16[8,600,420]{1,0,2:T(8,128)(2,1)} %param.4) | data formatting | bytes 8064000 | tf_op jit(solution)/shard_map/reshape | solution.py:39
  23.6 3.6 %fusion.20 = f32[224,4800]{1,0:T(8,128)S(1)} fusion(bf16[420,224]{0,1:T(8,128)(2,1)S(1)} %convert_element_type.96, bf16[4800,420]{0,1:T(8,128)(2,1)} %reshape.201), kind=kOutput, calls=%fused_computation.44 | convolution fusion | flops 903168000 | bytes 8520960 | tf_op jit(solution)/shard_map/dot_general | solution.py:18
  27.3 1.3 fusion.1
  28.6 3.8 %reshape.202 = bf16[8,600,224]{1,0,2:T(8,128)(2,1)} reshape(bf16[4800,224]{0,1:T(8,128)(2,1)S(1)} %fusion.1) | data formatting | bytes 4300800 | tf_op jit(solution)/shard_map/reshape | solution.py:41
  32.4 7.4 %all-to-all-start = ((bf16[8,600,224]{1,0,2:T(8,128)(2,1)}), bf16[8,600,224]{1,0,2:T(8,128)(2,1)S(1)}, u32[]{:S(2)}, u32[]{:S(2)}) async-start(bf16[8,600,224]{1,0,2:T(8,128)(2,1)} %reshape.202), calls=%async_computation | async-start | bytes 4587520 | tf_op jit(solution)/shard_map/all_to_all | solution.py:42
  39.9 0.2 all-reduce.2.cloned.1.call-start
  40.2 52.1 %all-to-all-done = bf16[8,600,224]{1,0,2:T(8,128)(2,1)S(1)} async-done(((bf16[8,600,224]{1,0,2:T(8,128)(2,1)}), bf16[8,600,224]{1,0,2:T(8,128)(2,1)S(1)}, u32[]{:S(2)}, u32[]{:S(2)}) %all-to-all-start) | async-done | bytes 2150432 | tf_op jit(solution)/shard_map/all_to_all | solution.py:42
  92.3 0.3 copy.20
  92.7 3.3 %convolution_bitcast_fusion.2 = f32[14,256,128]{1,2,0:T(8,128)S(1)} fusion(bf16[14,600,128]{1,2,0:T(8,128)(2,1)S(1)} %bitcast.74, bf16[14,600,256]{2,1,0:T(8,128)(2,1)} %param.6), kind=kOutput, calls=%fused_computation.15 | convolution fusion | flops 550502400 | bytes 8286208 | tf_op jit(solution)/shard_map/ksp,ksc->kpc/dot_general | solution.py:47
  96.0 0.9 convolution_bitcast_fusion.3
  97.0 1.1 multiply_reduce_fusion
  98.1 1.3 convolution_bitcast_fusion
  99.4 1.3 convolution_bitcast_fusion.1
  100.7 2.4 fusion.3
  103.2 1.2 pad_maximum_fusion
  104.4 3.4 %copy.25 = bf16[14,600,128]{1,2,0:T(8,128)(2,1)} copy(bf16[14,600,128]{2,1,0:T(8,128)(2,1)S(1)} %pad_maximum_fusion) | data formatting | bytes 4300800 | tf_op jit(solution)/shard_map/concatenate | solution.py:61
  107.8 53.8 %all-reduce.2.cloned.1.call-done = bf16[64,600,28]{1,0,2:T(8,128)(2,1)} async-done(((bf16[64,600,28]{1,0,2:T(8,128)(2,1)}), bf16[64,600,28]{1,0,2:T(8,128)(2,1)}) %all-reduce.2.cloned.1.call-update) | async-done | bytes 2150416 | tf_op jit(solution)/shard_map/psum | solution.py:68
  161.6 4.5 %copy.26 = bf16[64,600,28]{1,2,0:T(8,128)(2,1)} copy(bf16[64,600,28]{1,0,2:T(8,128)(2,1)} %all-reduce.2.cloned.1.call-done) | data formatting | bytes 4300800 | tf_op jit(solution)/shard_map/psum | solution.py:68
  166.0 5.5 %all-to-all-start.1 = ((bf16[64,600,28]{1,2,0:T(8,128)(2,1)}), bf16[64,600,28]{1,2,0:T(8,128)(2,1)S(1)}, u32[]{:S(2)}, u32[]{:S(2)}) async-start(bf16[64,600,28]{1,2,0:T(8,128)(2,1)} %copy.26), calls=%async_computation.1 | async-start | bytes 5242880 | tf_op jit(solution)/shard_map/all_to_all | solution.py:71
  171.6 8.0 %broadcast_multiply_fusion = (f32[420,112,1]{0,2,1:T(1,128)S(1)}, f32[420,112,1]{0,2,1:T(1,128)S(1)}) fusion(f32[112]{0:T(128)S(1)} %compare_select_fusion.1, f32[112]{0:T(128)S(1)} %broadcast_multiply_fusion.4), kind=kLoop, calls=%fused_computation.31 | loop fusion | flops 611520 | bytes 377216 | tf_op jit(solution)/shard_map/mul | solution.py:37
  179.6 0.4 pad_maximum_fusion.2
  180.1 0.3 reshape.208
  180.4 70.5 %psum.15 = f32[]{:T(128)} all-reduce(f32[]{:T(128)} %get-tuple-element.5), channel_id=1, replica_groups=mesh['par'=4,'freq'=8] {'par','freq'}, use_global_device_ids=true, to_apply=%region_2.3 | all-reduce | flops 1 | bytes 8 | tf_op jit(solution)/shard_map/psum | solution.py:55
  251.5 2.2 copy.33
  253.8 3.6 %reshape.207 = bf16[4800,224]{0,1:T(8,128)(2,1)S(1)} reshape(bf16[8,600,8,28]{1,0,3,2:T(8,128)(2,1)} %bitcast.83) | data formatting | bytes 4300800 | tf_op jit(solution)/shard_map/reshape | solution.py:72
  257.4 1.3 fusion.17
  258.6 4.6 %convolution_add_fusion = f32[4800,420]{0,1:T(8,128)} fusion(f32[4800,420]{0,1:T(8,128)S(1)} %fusion.17, bf16[4800,224]{0,1:T(8,128)(2,1)S(1)} %reshape.207, f32[420,224]{0,1:T(8,128)S(1)} %reshape.208), kind=kOutput, calls=%fused_computation.1 | convolution fusion | flops 905560320 | bytes 18654720 | tf_op jit(solution)/shard_map/dot_general | solution.py:18
  263.2 10.4 %reshape.209 = f32[8,600,420]{1,0,2:T(8,128)} reshape(f32[4800,420]{0,1:T(8,128)} %convolution_add_fusion) | data formatting | bytes 16128000 | tf_op jit(solution)/shard_map/reshape | solution.py:73
  273.6 7.7 %add_convert_fusion = bf16[8,600,420]{1,0,2:T(8,128)(2,1)} fusion(f32[8,600,420]{1,0,2:T(8,128)} %reshape.209, bf16[8,600,420]{1,0,2:T(8,128)(2,1)} %param.4, f32[]{:T(128)S(6)} %mul_shard_map.3), kind=kLoop, calls=%fused_computation | loop fusion | flops 8064000 | bytes 16128004 | tf_op jit(solution)/shard_map/convert_element_type | solution.py:74
  (22 shorter events, 0.5 us)
Async XLA Ops:
  23.6 3.6 %copy-start = (bf16[4800,420]{0,1:T(8,128)(2,1)S(1)}, bf16[4800,420]{0,1:T(8,128)(2,1)}, u32[]{:S(2)}) copy-start(bf16[4800,420]{0,1:T(8,128)(2,1)} %reshape.201) | copy-start | bytes 12096004
  28.6 11.5 %copy-start.1 = (f32[256]{0:T(256)S(1)}, f32[256]{0:T(256)}, u32[]{:S(2)}) copy-start(f32[256]{0:T(256)} %param.7) | copy-start | bytes 3076
  32.4 63.6 %slice-start.2 = ((s8[4300800]{0:T(1024)(128)(4,1)}), s8[106496]{0:T(1024)(128)(4,1)S(1)}, s32[]{:S(2)}) async-start(s8[4300800]{0:T(1024)(128)(4,1)} %bitcast.78), calls=%async_computation.5 | async-start | bytes 212992
  32.4 59.9 %all-to-all-start = ((bf16[8,600,224]{1,0,2:T(8,128)(2,1)}), bf16[8,600,224]{1,0,2:T(8,128)(2,1)S(1)}, u32[]{:S(2)}, u32[]{:S(2)}) async-start(bf16[8,600,224]{1,0,2:T(8,128)(2,1)} %reshape.202), calls=%async_computation | async-start | bytes 4587520 | tf_op jit(solution)/shard_map/all_to_all | solution.py:42
  39.9 121.7 %all-reduce.2.cloned.1.call-start = ((), (), s32[]{:S(2)}) async-start(), calls=%async_computation.2 | async-start | bytes 4587520 | tf_op jit(solution)/shard_map/psum | solution.py:68
  92.3 3.7 %slice-start.3 = ((s8[4300800]{0:T(1024)(128)(4,1)}), s8[4194304]{0:T(1024)(128)(4,1)S(1)}, s32[]{:S(2)}) async-start(s8[4300800]{0:T(1024)(128)(4,1)} %bitcast.78), calls=%async_computation.6 | async-start | bytes 8388608
  92.7 5.4 %slice-start = ((s8[4300800]{0:T(1024)(128)(4,1)}), s8[4194304]{0:T(1024)(128)(4,1)S(1)}, s32[]{:S(2)}) async-start(s8[4300800]{0:T(1024)(128)(4,1)} %bitcast.76), calls=%async_computation.3 | async-start | bytes 8388608
  96.0 2.0 slice-start.1
  166.0 85.5 %all-to-all-start.1 = ((bf16[64,600,28]{1,2,0:T(8,128)(2,1)}), bf16[64,600,28]{1,2,0:T(8,128)(2,1)S(1)}, u32[]{:S(2)}, u32[]{:S(2)}) async-start(bf16[64,600,28]{1,2,0:T(8,128)(2,1)} %copy.26), calls=%async_computation.1 | async-start | bytes 5242880 | tf_op jit(solution)/shard_map/all_to_all | solution.py:71
Sparse Core Ops, SparseCore 0:
  107.9 53.6 all-reduce.1
where the time goes:
time: 289 us; the launch traced here: 288 us
  waiting for transfers between devices  106 us (37%)
  blocking collectives  70.5 us (24%)
  local copies, waits for them, and re-layouts  36.9 us (13%)
  other arithmetic  29.7 us (10%)
  matrix products  17.7 us (6%)
  between operations  14.3 us (5%)
  starting transfers between devices  13.2 us (5%)
    psum x1, blocking collectives, shards(): lax.psum(quadratic, ('par', 'freq')) / (PROBES * SENSORS * STEPS)  70.5 us
    psum x1, waiting for transfers between devices, shards(): summed = lax.psum(w_partial.astype(jnp.bfloat16), 'par')  53.8 us
    all_to_all x1, waiting for transfers between devices, shards(): lax.all_to_all(spectrum, 'freq', split_axis=2, concat_axis=0, tiled=True)  52.1 us
    reshape x1, local copies, waits for them, and re-layouts, shards(): split_product(by_rows, inverse).reshape(probe_block, SENSORS, STEPS)  10.4 us
    mul x1, other arithmetic, shards(): -sines * all_weight[None, :]  8.04 us
    reshape x1, local copies, waits for them, and re-layouts, shards(): flattened = probes.reshape(probe_block * SENSORS, STEPS)  7.96 us
    neg x1, other arithmetic, shards(): -sines  7.81 us
    convert_element_type x1, other arithmetic, shards(): (response + noise_ratio * trace_est * probes.astype(jnp.float32)).astype(...  7.71 us
  transfers between devices with their start and end apart: 3, of which 2 were waited for; matrix products, arithmetic and copies ran while one was open for 3% of the time, Pallas kernels for 0%

commit v1 on v0

--- a/solution.py
+++ b/solution.py
@@ -1,6 +1,11 @@
+import functools
+
 import jax
 import jax.numpy as jnp
+import numpy as np
 from jax import lax
+from jax.experimental import pallas as pl
+from jax.experimental.pallas import tpu as pltpu
 from jax.sharding import PartitionSpec as P
 
 SENSORS = 600
@@ -20,7 +25,7 @@
     )
 
 
-def shards(probes, map_real, map_imag, prior_var):
+def plain_shards(probes, map_real, map_imag, prior_var):
     freq_count = lax.axis_size("freq")
     bins_dev = map_real.shape[0]
     probe_block = probes.shape[0]
@@ -74,6 +79,374 @@
     return (response + noise_ratio * trace_est * probes.astype(jnp.float32)).astype(jnp.bfloat16)
 
 
+MESH = pl.DeviceIdType.MESH
+ROWS = 16
+STAGES = 4
+F32, BF16 = jnp.float32, jnp.bfloat16
+
+
+def tables(steps, bins_dev, freq_count, par_count):
+    padded = STAGES * par_count
+    local = np.arange(padded)
+    bins = np.arange(freq_count)[:, None] * bins_dev + local[None, :]
+    angle = 2.0 * np.pi * ((bins[:, :, None] * np.arange(steps)) % PERIOD) / PERIOD
+    scale = (local < bins_dev)[None, :, None] / np.sqrt(PERIOD)
+    both = np.stack([np.cos(angle) * scale, -np.sin(angle) * scale], axis=2)
+    weight = np.where(bins == 0, 1.0, 2.0)[:, :, None, None]
+    forward = both.reshape(freq_count, par_count, STAGES, 2, steps).transpose(1, 2, 0, 3, 4)
+    forward = forward.reshape(par_count, STAGES * freq_count * 2, steps)
+    inverse = (both * weight).reshape(freq_count * padded * 2, steps)
+    return forward.astype(np.float32), inverse.astype(np.float32)
+
+
+def swap_matrix(outer, inner):
+    out = np.arange(outer * inner)
+    matrix = np.zeros((out.size, out.size), np.float32)
+    matrix[out, (out % outer) * inner + out // outer] = 1.0
+    return matrix
+
+
+def exchange_kernel(
+    freq_count, table_ref, swap_ref, prior_ref, probes_hbm, real_hbm, imag_hbm, y_hbm, trace_ref,
+    probes_v, real_v, imag_v, o_buf, s_buf, v_buf, w_buf, a_buf, h_buf, b_buf, q_buf, y_buf,
+    t_own, t_freq, t_mid, t_core, t_half, t_x,
+    load_sem, map_sem, out_sem, f_send, f_recv, g_send, g_recv, h_send, h_recv,
+    r_send, r_recv, rx_send, rx_recv, bf_send, bf_recv, bg_send, bg_recv, bh_send, bh_recv,
+    t_send, t_recv, tp_send, tp_recv,
+):
+    par, freq = lax.axis_index("par"), lax.axis_index("freq")
+    core, side = lax.rem(par, 2), par // 2
+    near = side * 2 + (1 - core)
+    across = (1 - side) * 2 + core
+    corner = (1 - side) * 2 + (1 - core)
+    bins_dev, sensors, params = real_v.shape
+    count = probes_v.shape[0]
+    pending = []
+
+    def send(src, dst, send_sem, recv_sem, par_to, freq_to):
+        copy = pltpu.make_async_remote_copy(
+            src_ref=src, dst_ref=dst, send_sem=send_sem, recv_sem=recv_sem,
+            device_id=(par_to, freq_to), device_id_type=MESH,
+        )
+        copy.start()
+        pending.append(copy)
+
+    def arrived(dst, sem):
+        pltpu.make_async_remote_copy(
+            src_ref=dst, dst_ref=dst, send_sem=sem, recv_sem=sem,
+            device_id=(near, freq), device_id_type=MESH,
+        ).wait_recv()
+
+    loads = [pltpu.make_async_copy(probes_hbm.at[r], probes_v.at[r], load_sem.at[r]) for r in range(count)]
+    for copy in loads:
+        copy.start()
+    maps = [
+        pltpu.make_async_copy(real_hbm, real_v, map_sem.at[0]),
+        pltpu.make_async_copy(imag_hbm, imag_v, map_sem.at[1]),
+    ]
+    for copy in maps:
+        copy.start()
+
+    barrier = pltpu.get_barrier_semaphore()
+    for d in range(1, freq_count):
+        pl.semaphore_signal(
+            barrier, inc=1, device_id=(par, lax.rem(freq + d, freq_count)), device_id_type=MESH
+        )
+    for other in (near, across):
+        pl.semaphore_signal(barrier, inc=1, device_id=(other, freq), device_id_type=MESH)
+
+    o_buf[...] = jnp.zeros_like(o_buf)
+    w_buf[...] = jnp.zeros_like(w_buf)
+    t_own[...] = jnp.zeros_like(t_own)
+    table = table_ref[par]
+    for r in range(count):
+        loads[r].wait()
+        rows = lax.dot_general(table, probes_v[r], (((1,), (1,)), ((), ())), preferred_element_type=F32)
+        o_buf[:, r, :, 0:sensors] = rows.astype(BF16).reshape(STAGES, ROWS, sensors)
+    width = o_buf.shape[-1]
+    swap = swap_ref[...]
+
+    def spread(i):
+        mixed = o_buf[i].reshape(count * ROWS, width)
+        mixed = jnp.dot(swap, mixed, preferred_element_type=F32).astype(BF16)
+        s_buf[i] = mixed.reshape(freq_count, ROWS, width)
+        v_buf[STAGES * par + i, freq] = s_buf[i, freq]
+
+    def send_spectra(i):
+        for d in range(1, freq_count):
+            to = lax.rem(freq + d, freq_count)
+            send(s_buf.at[i, to], v_buf.at[STAGES * par + i, freq], f_send.at[i, to], f_recv.at[i, freq], par, to)
+
+    def gather(i):
+        for d in range(1, freq_count):
+            src = lax.rem(freq + freq_count - d, freq_count)
+            arrived(v_buf.at[STAGES * par + i, src], f_recv.at[i, src])
+        block = v_buf.at[STAGES * par + i]
+        send(block, block, g_send.at[i, 0], g_recv.at[i, 0], across, freq)
+        send(block, block, g_send.at[i, 1], g_recv.at[i, 1], near, freq)
+
+    def gather_on(i):
+        block = v_buf.at[STAGES * across + i]
+        arrived(block, g_recv.at[i, 0])
+        send(block, block, h_send.at[i], h_recv.at[i], near, freq)
+
+    prior = prior_ref[...]
+
+    def compute(i):
+        arrived(v_buf.at[STAGES * near + i], g_recv.at[i, 1])
+        arrived(v_buf.at[STAGES * corner + i], h_recv.at[i])
+        if i == 0:
+            for copy in maps:
+                copy.wait()
+
+        def one(member, carry):
+            bin_at = STAGES * member + i
+
+            @pl.when(bin_at < bins_dev)
+            def _():
+                real, imag = real_v[bin_at], imag_v[bin_at]
+                v = v_buf[bin_at].reshape(freq_count * ROWS, width)[:, :sensors]
+                left = jnp.dot(v, real, preferred_element_type=F32).reshape(freq_count, 2, count, params)
+                right = jnp.dot(v, imag, preferred_element_type=F32).reshape(freq_count, 2, count, params)
+                u_real = left[:, 0] + right[:, 1]
+                u_imag = left[:, 1] - right[:, 0]
+                weight = jnp.where(freq * bins_dev + bin_at == 0, 1.0, 2.0).astype(F32)
+                t_own[...] += weight * prior * jnp.sum(u_real * u_real + u_imag * u_imag, axis=0)
+                scaled = jnp.stack([u_real * prior, u_imag * prior], axis=1)
+                scaled = scaled.reshape(freq_count * ROWS, params).astype(BF16)
+                turn = (((1,), (1,)), ((), ()))
+                left = lax.dot_general(scaled, real, turn, preferred_element_type=F32)
+                right = lax.dot_general(scaled, imag, turn, preferred_element_type=F32)
+                left = left.reshape(freq_count, 2, count, sensors)
+                right = right.reshape(freq_count, 2, count, sensors)
+                w = jnp.stack([left[:, 0] - right[:, 1], left[:, 1] + right[:, 0]], axis=1)
+                w_buf[bin_at, :, :, 0:sensors] = w.reshape(freq_count, ROWS, sensors).astype(BF16)
+
+            return carry
+
+        lax.fori_loop(0, 4, one, 0)
+        for s in range(2):
+            send(
+                w_buf.at[STAGES * (2 * s + 1 - core) + i], a_buf.at[s, i],
+                r_send.at[i, s], r_recv.at[i, s], near, freq,
+            )
+
+    def reduce_core(i):
+        for s in range(2):
+            arrived(a_buf.at[s, i], r_recv.at[i, s])
+        total = w_buf[STAGES * across + i].astype(F32) + a_buf[1 - side, i].astype(F32)
+        h_buf[i] = total.astype(BF16)
+        send(h_buf.at[i], b_buf.at[i], rx_send.at[i], rx_recv.at[i], across, freq)
+
+    def reduce_across(i):
+        arrived(b_buf.at[i], rx_recv.at[i])
+        total = w_buf[STAGES * par + i].astype(F32) + a_buf[side, i].astype(F32) + b_buf[i].astype(F32)
+        q_buf[i] = total.astype(BF16)
+        y_buf[freq, STAGES * par + i] = q_buf[i, freq]
+        for d in range(1, freq_count):
+            to = lax.rem(freq + d, freq_count)
+            send(q_buf.at[i, to], y_buf.at[freq, STAGES * par + i], bf_send.at[i, to], bf_recv.at[i, freq], par, to)
+
+    def back(i):
+        for d in range(1, freq_count):
+            src = lax.rem(freq + freq_count - d, freq_count)
+            arrived(y_buf.at[src, STAGES * par + i], bf_recv.at[i, src])
+        block = y_buf.at[:, STAGES * par + i]
+        send(block, block, bg_send.at[i, 0], bg_recv.at[i, 0], across, freq)
+        send(block, block, bg_send.at[i, 1], bg_recv.at[i, 1], near, freq)
+
+    def back_on(i):
+        block = y_buf.at[:, STAGES * across + i]
+        arrived(block, bg_recv.at[i, 0])
+        send(block, block, bh_send.at[i], bh_recv.at[i], near, freq)
+
+    def finish(i):
+        arrived(y_buf.at[:, STAGES * near + i], bg_recv.at[i, 1])
+        arrived(y_buf.at[:, STAGES * corner + i], bh_recv.at[i])
+
+    def trace_freq():
+        t_freq[freq] = t_own[...]
+        for d in range(1, freq_count):
+            to = lax.rem(freq + d, freq_count)
+            send(t_own, t_freq.at[freq], t_send.at[to], t_recv.at[freq], par, to)
+
+    def trace_core():
+        for d in range(1, freq_count):
+            src = lax.rem(freq + freq_count - d, freq_count)
+            arrived(t_freq.at[src], t_recv.at[src])
+        t_mid[...] = jnp.sum(t_freq[...], axis=0)
+        send(t_mid, t_core, tp_send.at[0], tp_recv.at[0], near, freq)
+
+    def trace_across():
+        arrived(t_core, tp_recv.at[0])
+        t_half[...] = t_mid[...] + t_core[...]
+        send(t_half, t_x, tp_send.at[1], tp_recv.at[1], across, freq)
+
+    spread(0)
+    pl.semaphore_wait(barrier, freq_count + 1)
+    send_spectra(0)
+    for i in range(1, STAGES):
+        spread(i)
+        send_spectra(i)
+    gather(0)
+    gather(1)
+    gather_on(0)
+    compute(0)
+    gather(2)
+    gather_on(1)
+    reduce_core(0)
+    compute(1)
+    gather(3)
+    gather_on(2)
+    reduce_core(1)
+    compute(2)
+    gather_on(3)
+    reduce_core(2)
+    reduce_across(0)
+    compute(3)
+    trace_freq()
+    reduce_core(3)
+    reduce_across(1)
+    trace_core()
+    back(0)
+    reduce_across(2)
+    trace_across()
+    back_on(0)
+    reduce_across(3)
+    back(1)
+    back_on(1)
+    back(2)
+    back_on(2)
+    back(3)
+    back_on(3)
+    for i in range(STAGES):
+        finish(i)
+    arrived(t_x, tp_recv.at[1])
+    trace_ref[...] = t_half[...] + t_x[...]
+    out = pltpu.make_async_copy(y_buf, y_hbm, out_sem)
+    out.start()
+    for copy in pending:
+        copy.wait_send()
+    out.wait()
+
+
+def inverse_kernel(factor, y_ref, trace_ref, swap_ref, table_ref, probes_ref, out_ref, x_buf):
+    at = pl.program_id(0)
+    freq_count, padded, rows, width = y_ref.shape
+    count = rows // 2
+    sensors = out_ref.shape[1]
+
+    @pl.when(at == 0)
+    def _():
+        swap = swap_ref[...]
+        for g in range(freq_count):
+            for h in range(padded // 8):
+                block = y_ref[g, 8 * h : 8 * h + 8].reshape(8 * rows, width)
+                block = jnp.dot(swap, block, preferred_element_type=F32).astype(BF16)
+                x_buf[:, g * (padded // 8) + h] = block.reshape(count, rows, width)
+
+    trace_est = jnp.sum(trace_ref[...]) * factor
+    block = x_buf[at].reshape(freq_count * padded * 2, width)
+    response = lax.dot_general(block, table_ref[...], (((0,), (0,)), ((), ())), preferred_element_type=F32)
+    response = response[:sensors]
+    out_ref[0] = (response + trace_est * probes_ref[0].astype(F32)).astype(BF16)
+
+
+def fast_shards(probes, map_real, map_imag, prior_var):
+    freq_count, par_count = lax.axis_size("freq"), lax.axis_size("par")
+    bins_dev, sensors, params = map_real.shape
+    count, _, steps = probes.shape
+    padded = STAGES * par_count
+    width = -(-sensors // 128) * 128
+    forward, inverse = tables(steps, bins_dev, freq_count, par_count)
+    forward, inverse = jnp.asarray(forward, BF16), jnp.asarray(inverse, BF16)
+    swap_out = jnp.asarray(swap_matrix(count, ROWS), BF16)
+    swap_in = jnp.asarray(swap_matrix(ROWS, count), BF16)
+    vmem, any_place = pl.BlockSpec(memory_space=pltpu.VMEM), pl.BlockSpec(memory_space=pl.ANY)
+    dma = pltpu.SemaphoreType.DMA
+    block = (freq_count, ROWS, width)
+    small = pltpu.VMEM((count, params), F32)
+    y, trace = pl.pallas_call(
+        functools.partial(exchange_kernel, freq_count),
+        out_shape=(
+            jax.ShapeDtypeStruct((freq_count, padded, ROWS, width), BF16),
+            jax.ShapeDtypeStruct((count, params), F32),
+        ),
+        in_specs=[vmem, vmem, vmem, any_place, any_place, any_place],
+        out_specs=(any_place, vmem),
+        scratch_shapes=[
+            pltpu.VMEM(probes.shape, BF16),
+            pltpu.VMEM(map_real.shape, BF16),
+            pltpu.VMEM(map_imag.shape, BF16),
+            pltpu.VMEM((STAGES, count, ROWS, width), BF16),
+            pltpu.VMEM((STAGES,) + block, BF16),
+            pltpu.VMEM((padded,) + block, BF16),
+            pltpu.VMEM((padded,) + block, BF16),
+            pltpu.VMEM((2, STAGES) + block, BF16),
+            pltpu.VMEM((STAGES,) + block, BF16),
+            pltpu.VMEM((STAGES,) + block, BF16),
+            pltpu.VMEM((STAGES,) + block, BF16),
+            pltpu.VMEM((freq_count, padded, ROWS, width), BF16),
+            small,
+            pltpu.VMEM((freq_count, count, params), F32),
+            small,
+            small,
+            small,
+            small,
+            dma((count,)),
+            dma((2,)),
+            dma,
+            dma((STAGES, freq_count)),
+            dma((STAGES, freq_count)),
+            dma((STAGES, 2)),
+            dma((STAGES, 2)),
+            dma((STAGES,)),
+            dma((STAGES,)),
+            dma((STAGES, 2)),
+            dma((STAGES, 2)),
+            dma((STAGES,)),
+            dma((STAGES,)),
+            dma((STAGES, freq_count)),
+            dma((STAGES, freq_count)),
+            dma((STAGES, 2)),
+            dma((STAGES, 2)),
+            dma((STAGES,)),
+            dma((STAGES,)),
+            dma((freq_count,)),
+            dma((freq_count,)),
+            dma((2,)),
+            dma((2,)),
+        ],
+        compiler_params=pltpu.CompilerParams(
+            collective_id=0, has_side_effects=True, vmem_limit_bytes=60 * 1024 * 1024
+        ),
+        name="exchange",
+    )(forward, swap_out, prior_var.reshape(1, params), probes, map_real, map_imag)
+    factor = noise_ratio / (count * freq_count * sensors * steps)
+    return pl.pallas_call(
+        functools.partial(inverse_kernel, factor),
+        grid=(count,),
+        out_shape=jax.ShapeDtypeStruct(probes.shape, BF16),
+        in_specs=[
+            pl.BlockSpec(y.shape, lambda r: (0, 0, 0, 0)),
+            pl.BlockSpec(trace.shape, lambda r: (0, 0)),
+            pl.BlockSpec(swap_in.shape, lambda r: (0, 0)),
+            pl.BlockSpec(inverse.shape, lambda r: (0, 0)),
+            pl.BlockSpec((1, sensors, steps), lambda r: (r, 0, 0)),
+        ],
+        out_specs=pl.BlockSpec((1, sensors, steps), lambda r: (r, 0, 0)),
+        scratch_shapes=[pltpu.VMEM((count, freq_count * padded // 8, ROWS, width), BF16)],
+        compiler_params=pltpu.CompilerParams(vmem_limit_bytes=48 * 1024 * 1024),
+        name="inverse",
+    )(y, trace, swap_in, inverse, probes)
+
+
+def shards(probes, map_real, map_imag, prior_var):
+    fits = lax.axis_size("par") == 4 and lax.axis_size("freq") == 8
+    fits = fits and probes.shape[0] == 8 and map_real.shape[0] <= 16
+    return (fast_shards if fits else plain_shards)(probes, map_real, map_imag, prior_var)
+
+
 def solution(mesh):
     placed = (P("freq", None, None), P("freq", None, "par"), P("freq", None, "par"), P("par"))
     return jax.shard_map(

time: 289 us -> 101 us (0.35)
  waiting for transfers between devices: 106 us -> 0 us
  Pallas kernels: 0 us -> 79.1 us
  blocking collectives: 70.5 us -> 0 us
  other arithmetic: 29.7 us -> 0 us
  matrix products: 17.7 us -> 0 us
  local copies, waits for them, and re-layouts: 36.9 us -> 19.8 us
  between operations: 14.3 us -> 0.04 us
  starting transfers between devices: 13.2 us -> 0 us
    pallas_call x0 -> x2, Pallas kernels: none -> 79.1 us  [the longest x1 70.2 us: fast_shards(): pl.pallas_call(functools.partial(exchange_kernel, freq_count), out_shape=...]
    psum x1 -> x0, blocking collectives: 70.5 us -> none  [shards(): lax.psum(quadratic, ('par', 'freq')) / (PROBES * SENSORS * STEPS)]
    psum x1 -> x0, waiting for transfers between devices: 53.8 us -> none  [shards(): summed = lax.psum(w_partial.astype(jnp.bfloat16), 'par')]
    all_to_all x2 -> x0, waiting for transfers between devices: 52.1 us -> none  [the longest x1 52.1 us: shards(): lax.all_to_all(spectrum, 'freq', split_axis=2, concat_axis=0, tiled=True)]
    reshape x5 -> x0, local copies, waits for them, and re-layouts: 26.1 us -> none  [the longest x1 10.4 us: shards(): split_product(by_rows, inverse).reshape(probe_block, SENSORS, STEPS)]
    dot_general x8 -> x0, matrix products: 17.7 us -> none  [the longest x2 5.9 us: split_product(): jnp.dot(left, lower, preferred_element_type=jnp.float32)]
    all_to_all x2 -> x0, starting transfers between devices: 13 us -> none  [the longest x1 7.44 us: shards(): lax.all_to_all(spectrum, 'freq', split_axis=2, concat_axis=0, tiled=True)]
    unnamed x12 -> x9, local copies, waits for them, and re-layouts: 0.03 us -> 10.8 us
  transfers between devices with their start and end apart: 3 -> 0, of which waited for: 2 -> 0; matrix products, arithmetic and copies ran while one was open for 3% -> 0% of each run, Pallas kernels for 0% -> 0%
where the time goes in v1:
time: 101 us; the launch traced here: 98.9 us
  Pallas kernels  79.1 us (78%)
  local copies, waits for them, and re-layouts  19.8 us (20%)
    pallas_call x1, Pallas kernels, fast_shards(): pl.pallas_call(functools.partial(exchange_kernel, freq_count), out_shape=...  70.2 us
    unnamed x9, local copies, waits for them, and re-layouts  10.8 us
    pallas_call x1, local copies, waits for them, and re-layouts, fast_shards(): pl.pallas_call(functools.partial(inverse_kernel, factor), grid=(count,),...  9.01 us
    pallas_call x1, Pallas kernels, fast_shards(): pl.pallas_call(functools.partial(inverse_kernel, factor), grid=(count,),...  8.92 us

profile of v1, /device:TPU:0, one launch (start us, length us, event | category | flops | bytes accessed | tf_op | source)
XLA Modules:
  0.0 98.9 jit_solution(2745644487495723712)
XLA Ops:
  0.0 8.4 %copy.9.probes_hbm.probes_ref = bf16[8,600,420]{2,1,0:T(8,128)(2,1)} copy(bf16[8,600,420]{1,0,2:T(8,128)(2,1)} %param.8) | data formatting | bytes 8064000 | tf_op args[0]
  8.4 0.0 copy-start.1
  8.4 0.0 copy-start.2
  8.4 70.2 %exchange.1 = (bf16[8,16,16,640]{3,2,1,0:T(8,128)(2,1)}, f32[8,256]{1,0:T(8,128)}) custom-call(bf16[4,64,420]{2,1,0:T(8,128)(2,1)} %constant.8.clone.table_ref, bf16[128,128]{1,0:T(8,128)(2,1)} %constant.10.clone.swap_ref, f32[1,256]{1,0:T(1,128)} %bitcast.1, bf16[8,600,420]{2,1,0:T(8,128)(2,1)} %copy.9.probes_hbm.probes_ref, ...), custom_call_target="tpu_custom_call" | custom-call | tf_op jit(solution)/shard_map/exchange/pallas_call | solution.py:369
  78.6 0.0 copy-done.1
  78.6 0.0 copy-done.2
  78.6 0.0 copy-start
  78.6 1.7 %copy-done = bf16[8,16,16,640]{3,2,1,0:T(8,128)(2,1)S(1)} copy-done((bf16[8,16,16,640]{3,2,1,0:T(8,128)(2,1)S(1)}, bf16[8,16,16,640]{3,2,1,0:T(8,128)(2,1)}, u32[]{:S(2)}) %copy-start) | copy-done | bytes 2621464
  80.3 0.0 copy-start.3
  80.3 0.7 copy-done.3
  81.0 8.9 %inverse.1 = bf16[8,600,420]{2,1,0:T(8,128)(2,1)} custom-call(bf16[8,16,16,640]{3,2,1,0:T(8,128)(2,1)S(1)} %copy-done, f32[8,256]{1,0:T(8,128)S(1)} %copy-done.3, bf16[128,128]{1,0:T(8,128)(2,1)S(1)} %copy-done.2, bf16[256,420]{1,0:T(8,128)(2,1)S(1)} %copy-done.1, bf16[8,600,420]{2,1,0:T(8,128)(2,1)} %copy.9.probes_hbm.probes_ref), custom_call_target="tpu_custom_call" | custom-call | tf_op jit(solution)/shard_map/inverse/pallas_call | solution.py:426
  89.9 9.0 %copy.11 = bf16[8,600,420]{1,0,2:T(8,128)(2,1)} copy(bf16[8,600,420]{2,1,0:T(8,128)(2,1)} %inverse.1) | data formatting | bytes 8064000 | tf_op jit(solution)/shard_map/inverse/pallas_call | solution.py:426
Async XLA Ops:
  8.4 70.2 %copy-start.1 = (bf16[256,420]{1,0:T(8,128)(2,1)S(1)}, bf16[256,420]{1,0:T(8,128)(2,1)}, u32[]{:S(2)}) copy-start(bf16[256,420]{1,0:T(8,128)(2,1)} %constant.9.clone.table_ref) | copy-start | bytes 645124
  8.4 70.2 %copy-start.2 = (bf16[128,128]{1,0:T(8,128)(2,1)S(1)}, bf16[128,128]{1,0:T(8,128)(2,1)}, u32[]{:S(2)}) copy-start(bf16[128,128]{1,0:T(8,128)(2,1)} %constant.11.clone.swap_ref) | copy-start | bytes 98308
  78.6 1.7 %copy-start = (bf16[8,16,16,640]{3,2,1,0:T(8,128)(2,1)S(1)}, bf16[8,16,16,640]{3,2,1,0:T(8,128)(2,1)}, u32[]{:S(2)}) copy-start(bf16[8,16,16,640]{3,2,1,0:T(8,128)(2,1)} %get-tuple-element.7.y_ref) | copy-start | bytes 7864324
  80.3 0.7 copy-start.3

commit v2 on v0

--- a/solution.py
+++ b/solution.py
@@ -1,6 +1,11 @@
+import functools
+
 import jax
 import jax.numpy as jnp
+import numpy as np
 from jax import lax
+from jax.experimental import pallas as pl
+from jax.experimental.pallas import tpu as pltpu
 from jax.sharding import PartitionSpec as P
 
 SENSORS = 600
@@ -20,7 +25,7 @@
     )
 
 
-def shards(probes, map_real, map_imag, prior_var):
+def plain_shards(probes, map_real, map_imag, prior_var):
     freq_count = lax.axis_size("freq")
     bins_dev = map_real.shape[0]
     probe_block = probes.shape[0]
@@ -74,6 +79,453 @@
     return (response + noise_ratio * trace_est * probes.astype(jnp.float32)).astype(jnp.bfloat16)
 
 
+MESH = pl.DeviceIdType.MESH
+ROWS = 16
+GROUP = 4
+F32, BF16 = jnp.float32, jnp.bfloat16
+
+
+def stage_members(stage, bins_dev):
+    return (0, 1, 2, 3) if bins_dev - GROUP * stage >= GROUP else (0, 3)
+
+
+def tables(steps, bins_dev, freq_count):
+    stages = -(-bins_dev // GROUP)
+    bins = np.arange(freq_count * bins_dev)
+    angle = 2.0 * np.pi * ((bins[:, None] * np.arange(steps)) % PERIOD) / PERIOD
+    both = np.stack([np.cos(angle), -np.sin(angle)], axis=1) / np.sqrt(PERIOD)
+    weighted = both * np.where(bins == 0, 1.0, 2.0)[:, None, None]
+    both = both.reshape(freq_count, bins_dev, 2, steps)
+    weighted = weighted.reshape(freq_count, bins_dev, 2, steps)
+    forward = np.zeros((GROUP, stages, freq_count, 2, steps))
+    inverse = []
+    for stage in range(stages):
+        members = stage_members(stage, bins_dev)
+        for n, member in enumerate(members):
+            forward[member, stage] = both[:, GROUP * stage + n]
+        inverse.append(weighted[:, GROUP * stage : GROUP * stage + len(members)].reshape(-1, steps))
+    forward = forward.reshape(GROUP, stages * freq_count * 2, steps)
+    return forward.astype(np.float32), np.concatenate(inverse).astype(np.float32)
+
+
+def swap_matrix(outer, inner):
+    out = np.arange(outer * inner)
+    matrix = np.zeros((out.size, out.size), np.float32)
+    matrix[out, (out % outer) * inner + out // outer] = 1.0
+    return matrix
+
+
+def exchange_kernel(
+    freq_count, table_ref, swap_ref, back_ref, prior_ref, probes_hbm, real_hbm, imag_hbm, x_hbm, trace_ref,
+    probes_v, split_v, real_v, imag_v, o_buf, s_buf, v_buf, w_buf, a_buf, h_buf, b_buf, q_buf, y_buf, x_buf,
+    t_own, t_freq, t_mid, t_core, t_half, t_x,
+    load_sem, map_sem, out_sem, f_send, f_recv, g_send, g_recv, h_send, h_recv,
+    r_send, r_recv, rx_send, rx_recv, bf_send, bf_recv, bg_send, bg_recv, bh_send, bh_recv,
+    t_send, t_recv, tp_send, tp_recv,
+):
+    par, freq = lax.axis_index("par"), lax.axis_index("freq")
+    core, side = lax.rem(par, 2), par // 2
+    near = side * 2 + (1 - core)
+    across = (1 - side) * 2 + core
+    corner = (1 - side) * 2 + (1 - core)
+    bins_dev, sensors, params = real_v.shape
+    steps, count = probes_v.shape[:2]
+    stages, width = o_buf.shape[0], o_buf.shape[-1]
+    lanes = [(128 * j, min(128, sensors - 128 * j)) for j in range(width // 128)]
+    outer = core == side
+    inner = core != side
+    pending = []
+
+    def when(i, condition, body):
+        if len(stage_members(i, bins_dev)) == GROUP:
+            body()
+        else:
+            pl.when(condition)(body)
+
+    def send(i, condition, make):
+        make().start()
+        pending.append((i, condition, make))
+
+    def remote(src, dst, send_sem, recv_sem, par_to, freq_to):
+        return pltpu.make_async_remote_copy(
+            src_ref=src, dst_ref=dst, send_sem=send_sem, recv_sem=recv_sem,
+            device_id=(par_to, freq_to), device_id_type=MESH,
+        )
+
+    def arrived(dst, sem):
+        remote(dst, dst, sem, sem, near, freq).wait_recv()
+
+    pieces = load_sem.shape[0]
+    piece = steps // pieces
+    loads = [
+        pltpu.make_async_copy(
+            probes_hbm.at[pl.ds(n * piece, piece)], probes_v.at[pl.ds(n * piece, piece)], load_sem.at[n]
+        )
+        for n in range(pieces)
+    ]
+    for copy in loads:
+        copy.start()
+    maps = [
+        pltpu.make_async_copy(real_hbm, real_v, map_sem.at[0]),
+        pltpu.make_async_copy(imag_hbm, imag_v, map_sem.at[1]),
+    ]
+    for copy in maps:
+        copy.start()
+
+    def peer(d):
+        return lax.rem(freq + d, freq_count)
+
+    barrier = pltpu.get_barrier_semaphore()
+    for d in range(1, freq_count):
+        pl.semaphore_signal(barrier, inc=1, device_id=(par, peer(d)), device_id_type=MESH)
+    for other in (near, across):
+        pl.semaphore_signal(barrier, inc=1, device_id=(other, freq), device_id_type=MESH)
+
+    o_buf[...] = jnp.zeros_like(o_buf)
+    w_buf[...] = jnp.zeros_like(w_buf)
+    t_own[...] = jnp.zeros_like(t_own)
+    split_v[len(lanes) - 1] = jnp.zeros_like(split_v[len(lanes) - 1])
+    for n in range(pieces):
+        loads[n].wait()
+        rows = probes_v[n * piece : (n + 1) * piece].astype(F32).reshape(piece * count, sensors)
+        for j, (start, size) in enumerate(lanes):
+            split_v[j, n * piece * count : (n + 1) * piece * count, 0:size] = rows[:, start : start + size]
+    table = table_ref[par]
+    for r in range(count):
+        one = [split_v[j, pl.ds(r, steps, stride=count), :].astype(BF16) for j in range(len(lanes))]
+        rows = jnp.dot(table, jnp.concatenate(one, axis=1), preferred_element_type=F32)
+        o_buf[:, r] = rows.astype(BF16).reshape(stages, ROWS, width)
+    swap = swap_ref[...]
+
+    def spread(i):
+        mixed = o_buf[i].reshape(count * ROWS, width)
+        mixed = jnp.dot(swap, mixed, preferred_element_type=F32).astype(BF16)
+        s_buf[i] = mixed.reshape(freq_count, ROWS, width)
+        v_buf[stages * par + i, freq] = s_buf[i, freq]
+
+    def send_spectra(i):
+        def body():
+            for d in range(1, freq_count):
+                send(i, outer, lambda d=d: remote(
+                    s_buf.at[i, peer(d)], v_buf.at[stages * par + i, freq],
+                    f_send.at[i, peer(d)], f_recv.at[i, freq], par, peer(d),
+                ))
+
+        when(i, outer, body)
+
+    def gather(i):
+        def body():
+            for d in range(1, freq_count):
+                src = peer(freq_count - d)
+                arrived(v_buf.at[stages * par + i, src], f_recv.at[i, src])
+            for k, to in enumerate((across, near)):
+                send(i, outer, lambda k=k, to=to: remote(
+                    v_buf.at[stages * par + i], v_buf.at[stages * par + i],
+                    g_send.at[i, k], g_recv.at[i, k], to, freq,
+                ))
+
+        when(i, outer, body)
+
+    def gather_on(i):
+        def body():
+            arrived(v_buf.at[stages * across + i], g_recv.at[i, 0])
+            send(i, inner, lambda: remote(
+                v_buf.at[stages * across + i], v_buf.at[stages * across + i],
+                h_send.at[i], h_recv.at[i], near, freq,
+            ))
+
+        when(i, inner, body)
+
+    prior = prior_ref[...]
+
+    def compute(i):
+        members = stage_members(i, bins_dev)
+        when(i, inner, lambda: arrived(v_buf.at[stages * near + i], g_recv.at[i, 1]))
+        when(i, outer, lambda: arrived(v_buf.at[stages * corner + i], h_recv.at[i]))
+        if i == 0:
+            for copy in maps:
+                copy.wait()
+
+        def one(n, carry):
+            slot = stages * n * ((GROUP - 1) // (len(members) - 1)) + i
+            bin_at = GROUP * i + n
+            real, imag = real_v[bin_at], imag_v[bin_at]
+            v = v_buf[slot].reshape(freq_count * ROWS, width)[:, :sensors]
+            left = jnp.dot(v, real, preferred_element_type=F32).reshape(freq_count, 2, count, params)
+            right = jnp.dot(v, imag, preferred_element_type=F32).reshape(freq_count, 2, count, params)
+            u_real = left[:, 0] + right[:, 1]
+            u_imag = left[:, 1] - right[:, 0]
+            weight = jnp.where(freq * bins_dev + bin_at == 0, 1.0, 2.0).astype(F32)
+            t_own[...] += weight * prior * jnp.sum(u_real * u_real + u_imag * u_imag, axis=0)
+            scaled = jnp.stack([u_real * prior, u_imag * prior], axis=1)
+            scaled = scaled.reshape(freq_count * ROWS, params).astype(BF16)
+            turn = (((1,), (1,)), ((), ()))
+            left = lax.dot_general(scaled, real, turn, preferred_element_type=F32)
+            right = lax.dot_general(scaled, imag, turn, preferred_element_type=F32)
+            left = left.reshape(freq_count, 2, count, sensors)
+            right = right.reshape(freq_count, 2, count, sensors)
+            w = jnp.stack([left[:, 0] - right[:, 1], left[:, 1] + right[:, 0]], axis=1)
+            w_buf[slot, :, :, 0:sensors] = w.reshape(freq_count, ROWS, sensors).astype(BF16)
+            return carry
+
+        lax.fori_loop(0, len(members), one, 0)
+
+        def give(owner, owner_side, condition):
+            def body():
+                send(i, condition, lambda: remote(
+                    w_buf.at[stages * owner + i], a_buf.at[owner_side, i],
+                    r_send.at[i, owner_side], r_recv.at[i, owner_side], near, freq,
+                ))
+
+            when(i, condition, body)
+
+        give(corner, 1 - side, outer)
+        give(near, side, inner)
+
+    def reduce_core(i):
+        def body():
+            arrived(a_buf.at[1 - side, i], r_recv.at[i, 1 - side])
+            total = w_buf[stages * across + i].astype(F32) + a_buf[1 - side, i].astype(F32)
+            h_buf[i] = total.astype(BF16)
+            send(i, inner, lambda: remote(h_buf.at[i], b_buf.at[i], rx_send.at[i], rx_recv.at[i], across, freq))
+
+        when(i, inner, body)
+
+    def reduce_across(i):
+        def body():
+            arrived(a_buf.at[side, i], r_recv.at[i, side])
+            arrived(b_buf.at[i], rx_recv.at[i])
+            total = w_buf[stages * par + i].astype(F32) + a_buf[side, i].astype(F32) + b_buf[i].astype(F32)
+            q_buf[i] = total.astype(BF16)
+            y_buf[freq, stages * par + i] = q_buf[i, freq]
+            for d in range(1, freq_count):
+                send(i, outer, lambda d=d: remote(
+                    q_buf.at[i, peer(d)], y_buf.at[freq, stages * par + i],
+                    bf_send.at[i, peer(d)], bf_recv.at[i, freq], par, peer(d),
+                ))
+
+        when(i, outer, body)
+
+    def back(i):
+        def body():
+            for d in range(1, freq_count):
+                src = peer(freq_count - d)
+                arrived(y_buf.at[src, stages * par + i], bf_recv.at[i, src])
+            for k, to in enumerate((across, near)):
+                send(i, outer, lambda k=k, to=to: remote(
+                    y_buf.at[:, stages * par + i], y_buf.at[:, stages * par + i],
+                    bg_send.at[i, k], bg_recv.at[i, k], to, freq,
+                ))
+
+        when(i, outer, body)
+
+    def back_on(i):
+        def body():
+            arrived(y_buf.at[:, stages * across + i], bg_recv.at[i, 0])
+            send(i, inner, lambda: remote(
+                y_buf.at[:, stages * across + i], y_buf.at[:, stages * across + i],
+                bh_send.at[i], bh_recv.at[i], near, freq,
+            ))
+
+        when(i, inner, body)
+
+    turn_back = back_ref[...]
+    outs = []
+
+    def finish(i):
+        when(i, inner, lambda: arrived(y_buf.at[:, stages * near + i], bg_recv.at[i, 1]))
+        when(i, outer, lambda: arrived(y_buf.at[:, stages * corner + i], bh_recv.at[i]))
+        members = stage_members(i, bins_dev)
+        slabs = [(g, stages * m + i) for g in range(freq_count) for m in members]
+        first = GROUP * i * freq_count // 8
+        for b in range(len(slabs) // 8):
+            block = jnp.concatenate([y_buf[g, slot] for g, slot in slabs[8 * b : 8 * b + 8]], axis=0)
+            block = jnp.dot(turn_back, block, preferred_element_type=F32).astype(BF16)
+            x_buf[:, first + b] = block.reshape(count, ROWS, width)
+        part = pl.ds(first, len(slabs) // 8)
+        outs.append(pltpu.make_async_copy(x_buf.at[:, part], x_hbm.at[:, part], out_sem.at[i]))
+        outs[-1].start()
+
+    def trace_freq():
+        t_freq[freq] = t_own[...]
+        for d in range(1, freq_count):
+            send(0, None, lambda d=d: remote(
+                t_own, t_freq.at[freq], t_send.at[peer(d)], t_recv.at[freq], par, peer(d)
+            ))
+
+    def trace_core():
+        for d in range(1, freq_count):
+            src = peer(freq_count - d)
+            arrived(t_freq.at[src], t_recv.at[src])
+        t_mid[...] = jnp.sum(t_freq[...], axis=0)
+        send(0, None, lambda: remote(t_mid, t_core, tp_send.at[0], tp_recv.at[0], near, freq))
+
+    def trace_across():
+        arrived(t_core, tp_recv.at[0])
+        t_half[...] = t_mid[...] + t_core[...]
+        send(0, None, lambda: remote(t_half, t_x, tp_send.at[1], tp_recv.at[1], across, freq))
+
+    last = stages - 1
+    spread(0)
+    pl.semaphore_wait(barrier, freq_count + 1)
+    send_spectra(0)
+    for i in range(1, stages):
+        spread(i)
+        send_spectra(i)
+    gather(0)
+    for i in range(stages):
+        if i < last:
+            gather(i + 1)
+        gather_on(i)
+        if i > 0:
+            reduce_core(i - 1)
+        if i > 2:
+            reduce_across(i - 3)
+        compute(i)
+    trace_freq()
+    reduce_core(last)
+    for i in range(max(last - 2, 0), last):
+        reduce_across(i)
+    trace_core()
+    back(0)
+    reduce_across(last)
+    trace_across()
+    back_on(0)
+    for i in range(1, stages):
+        back(i)
+        finish(i - 1)
+        back_on(i)
+    finish(last)
+    arrived(t_x, tp_recv.at[1])
+    trace_ref[...] = t_half[...] + t_x[...]
+    for i, condition, make in pending:
+        when(i, condition, lambda make=make: make().wait_send())
+    for copy in outs:
+        copy.wait()
+
+
+def inverse_kernel(factor, x_ref, trace_ref, table_ref, probes_ref, out_ref, split_v):
+    count, blocks, rows, width = x_ref.shape
+    piece, _, sensors = out_ref.shape
+    table = table_ref[0]
+    trace_est = jnp.sum(trace_ref[...]) * factor
+    for r in range(count):
+        block = x_ref[r].reshape(blocks * rows, width)
+        response = jnp.dot(table, block, preferred_element_type=F32)
+        for j in range(width // 128):
+            split_v[j, pl.ds(r, piece, stride=count), :] = response[:, 128 * j : 128 * j + 128]
+    for j in range(width // 128):
+        start, size = 128 * j, min(128, sensors - 128 * j)
+        part = split_v[j].reshape(piece, count, 128)[:, :, :size]
+        noise = trace_est * probes_ref[:, :, start : start + size].astype(F32)
+        out_ref[:, :, start : start + size] = (part + noise).astype(BF16)
+
+
+def fast_shards(probes, map_real, map_imag, prior_var):
+    freq_count = lax.axis_size("freq")
+    bins_dev, sensors, params = map_real.shape
+    count, _, steps = probes.shape
+    stages = -(-bins_dev // GROUP)
+    padded = stages * GROUP
+    width = -(-sensors // 128) * 128
+    pieces = next(n for n in (3, 4, 5, 2, 1) if steps % n == 0)
+    forward, inverse = tables(steps, bins_dev, freq_count)
+    blocks = inverse.shape[0] // ROWS
+    inverse = jnp.asarray(inverse.T.reshape(pieces, steps // pieces, -1), BF16)
+    forward = jnp.asarray(forward, BF16)
+    swap_out = jnp.asarray(swap_matrix(count, ROWS), BF16)
+    swap_in = jnp.asarray(swap_matrix(ROWS, count), BF16)
+    by_time = probes.transpose(2, 0, 1)
+    vmem, any_place = pl.BlockSpec(memory_space=pltpu.VMEM), pl.BlockSpec(memory_space=pl.ANY)
+    dma = pltpu.SemaphoreType.DMA
+    block = (freq_count, ROWS, width)
+    small = pltpu.VMEM((count, params), F32)
+    staged = pltpu.VMEM((stages,) + block, BF16)
+    peers, pairs, single = dma((stages, freq_count)), dma((stages, 2)), dma((stages,))
+    x, trace = pl.pallas_call(
+        functools.partial(exchange_kernel, freq_count),
+        out_shape=(
+            jax.ShapeDtypeStruct((count, blocks, ROWS, width), BF16),
+            jax.ShapeDtypeStruct((count, params), F32),
+        ),
+        in_specs=[vmem, vmem, vmem, vmem, any_place, any_place, any_place],
+        out_specs=(any_place, vmem),
+        scratch_shapes=[
+            pltpu.VMEM(by_time.shape, BF16),
+            pltpu.VMEM((width // 128, steps * count, 128), F32),
+            pltpu.VMEM(map_real.shape, BF16),
+            pltpu.VMEM(map_imag.shape, BF16),
+            pltpu.VMEM((stages, count, ROWS, width), BF16),
+            staged,
+            pltpu.VMEM((padded,) + block, BF16),
+            pltpu.VMEM((padded,) + block, BF16),
+            pltpu.VMEM((2, stages) + block, BF16),
+            staged,
+            staged,
+            staged,
+            pltpu.VMEM((freq_count, padded, ROWS, width), BF16),
+            pltpu.VMEM((count, blocks, ROWS, width), BF16),
+            small,
+            pltpu.VMEM((freq_count, count, params), F32),
+            small,
+            small,
+            small,
+            small,
+            dma((pieces,)),
+            dma((2,)),
+            single,
+            peers,
+            peers,
+            pairs,
+            pairs,
+            single,
+            single,
+            pairs,
+            pairs,
+            single,
+            single,
+            peers,
+            peers,
+            pairs,
+            pairs,
+            single,
+            single,
+            dma((freq_count,)),
+            dma((freq_count,)),
+            dma((2,)),
+            dma((2,)),
+        ],
+        compiler_params=pltpu.CompilerParams(
+            collective_id=0, has_side_effects=True, vmem_limit_bytes=60 * 1024 * 1024
+        ),
+        name="exchange",
+    )(forward, swap_out, swap_in, prior_var.reshape(1, params), by_time, map_real, map_imag)
+    factor = noise_ratio / (count * freq_count * sensors * steps)
+    piece = steps // pieces
+    result = pl.pallas_call(
+        functools.partial(inverse_kernel, factor),
+        grid=(pieces,),
+        out_shape=jax.ShapeDtypeStruct(by_time.shape, BF16),
+        in_specs=[
+            pl.BlockSpec(x.shape, lambda n: (0, 0, 0, 0)),
+            pl.BlockSpec(trace.shape, lambda n: (0, 0)),
+            pl.BlockSpec((1, piece, blocks * ROWS), lambda n: (n, 0, 0)),
+            pl.BlockSpec((piece, count, sensors), lambda n: (n, 0, 0)),
+        ],
+        out_specs=pl.BlockSpec((piece, count, sensors), lambda n: (n, 0, 0)),
+        scratch_shapes=[pltpu.VMEM((width // 128, piece * count, 128), F32)],
+        compiler_params=pltpu.CompilerParams(vmem_limit_bytes=48 * 1024 * 1024),
+        name="inverse",
+    )(x, trace, inverse, by_time)
+    return result.transpose(1, 2, 0)
+
+
+def shards(probes, map_real, map_imag, prior_var):
+    fits = lax.axis_size("par") == GROUP and lax.axis_size("freq") == 8
+    fits = fits and probes.shape[0] == 8 and map_real.shape[0] % 4 in (0, 2) and map_real.shape[0] > 8
+    return (fast_shards if fits else plain_shards)(probes, map_real, map_imag, prior_var)
+
+
 def solution(mesh):
     placed = (P("freq", None, None), P("freq", None, "par"), P("freq", None, "par"), P("par"))
     return jax.shard_map(

time: 289 us -> 77.8 us (0.27)
  the two profiles are of different devices: /device:TPU:0 before, /device:TPU:19 now
where the time goes in v2:
time: 77.8 us; the launch traced here: 77.5 us
  Pallas kernels  75.1 us (97%)
  local copies, waits for them, and re-layouts  2.34 us (3%)
    pallas_call x1, Pallas kernels, fast_shards(): pl.pallas_call(functools.partial(exchange_kernel, freq_count), out_shape=...  68.3 us
    pallas_call x1, Pallas kernels, fast_shards(): pl.pallas_call(functools.partial(inverse_kernel, factor), grid=(pieces,),...  6.83 us
    unnamed x6, local copies, waits for them, and re-layouts  2.34 us

profile of v2, /device:TPU:19, one launch (start us, length us, event | category | flops | bytes accessed | tf_op | source)
XLA Modules:
  0.0 77.5 jit_solution(1826821655968821862)
XLA Ops:
  0.0 0.0 copy-start.1
  0.0 68.3 %exchange.1 = (bf16[8,14,16,640]{3,2,1,0:T(8,128)(2,1)}, f32[8,256]{1,0:T(8,128)}) custom-call(bf16[4,64,420]{2,1,0:T(8,128)(2,1)} %constant.9.clone.table_ref, bf16[128,128]{1,0:T(8,128)(2,1)} %constant.10.clone.swap_ref, bf16[128,128]{1,0:T(8,128)(2,1)} %constant.11.clone.back_ref, f32[1,256]{1,0:T(1,128)} %bitcast.5, bf16[420,8,600]{2,1,0:T(8,128)(2,1)} %bitcast.3, ...), custom_call_target="tpu_custom_call" | custom-call | tf_op jit(solution)/shard_map/exchange/pallas_call | solution.py:445
  68.3 0.0 copy-done.1
  68.3 0.0 copy-start
  68.3 1.6 %copy-done = bf16[8,14,16,640]{3,2,1,0:T(8,128)(2,1)S(1)} copy-done((bf16[8,14,16,640]{3,2,1,0:T(8,128)(2,1)S(1)}, bf16[8,14,16,640]{3,2,1,0:T(8,128)(2,1)}, u32[]{:S(2)}) %copy-start) | copy-done | bytes 2293784
  70.0 0.0 copy-start.2
  70.0 0.7 copy-done.2
  70.7 6.8 %inverse.1 = bf16[420,8,600]{2,1,0:T(8,128)(2,1)} custom-call(bf16[8,14,16,640]{3,2,1,0:T(8,128)(2,1)S(1)} %copy-done, f32[8,256]{1,0:T(8,128)S(1)} %copy-done.2, bf16[3,140,224]{2,1,0:T(8,128)(2,1)S(1)} %copy-done.1, bf16[420,8,600]{2,1,0:T(8,128)(2,1)} %bitcast.4), custom_call_target="tpu_custom_call" | custom-call | tf_op jit(solution)/shard_map/inverse/pallas_call | solution.py:505
Async XLA Ops:
  0.0 68.3 %copy-start.1 = (bf16[3,140,224]{2,1,0:T(8,128)(2,1)S(1)}, bf16[3,140,224]{2,1,0:T(8,128)(2,1)}, u32[]{:S(2)}) copy-start(bf16[3,140,224]{2,1,0:T(8,128)(2,1)} %constant.8.clone.table_ref) | copy-start | bytes 564484
  68.3 1.6 %copy-start = (bf16[8,14,16,640]{3,2,1,0:T(8,128)(2,1)S(1)}, bf16[8,14,16,640]{3,2,1,0:T(8,128)(2,1)}, u32[]{:S(2)}) copy-start(bf16[8,14,16,640]{3,2,1,0:T(8,128)(2,1)} %get-tuple-element.7.x_ref) | copy-start | bytes 6881284
  70.0 0.7 copy-start.2

commit v3 on v2

--- a/solution.py
+++ b/solution.py
@@ -169,8 +169,6 @@
         pltpu.make_async_copy(real_hbm, real_v, map_sem.at[0]),
         pltpu.make_async_copy(imag_hbm, imag_v, map_sem.at[1]),
     ]
-    for copy in maps:
-        copy.start()
 
     def peer(d):
         return lax.rem(freq + d, freq_count)
@@ -190,6 +188,8 @@
         rows = probes_v[n * piece : (n + 1) * piece].astype(F32).reshape(piece * count, sensors)
         for j, (start, size) in enumerate(lanes):
             split_v[j, n * piece * count : (n + 1) * piece * count, 0:size] = rows[:, start : start + size]
+    for copy in maps:
+        copy.start()
     table = table_ref[par]
     for r in range(count):
         one = [split_v[j, pl.ds(r, steps, stride=count), :].astype(BF16) for j in range(len(lanes))]
@@ -376,25 +376,30 @@
     for i in range(stages):
         if i < last:
             gather(i + 1)
+        if i > 2:
+            reduce_across(i - 3)
         gather_on(i)
         if i > 0:
             reduce_core(i - 1)
-        if i > 2:
-            reduce_across(i - 3)
         compute(i)
     trace_freq()
     reduce_core(last)
-    for i in range(max(last - 2, 0), last):
+    first = max(last - 2, 0)
+    for i in range(first, last):
         reduce_across(i)
+        if i == first:
+            back(0)
+    reduce_across(last)
     trace_core()
-    back(0)
-    reduce_across(last)
-    trace_across()
-    back_on(0)
     for i in range(1, stages):
         back(i)
-        finish(i - 1)
-        back_on(i)
+        if i > 1:
+            finish(i - 2)
+        back_on(i - 1)
+        if i == 1:
+            trace_across()
+    finish(last - 1)
+    back_on(last)
     finish(last)
     arrived(t_x, tp_recv.at[1])
     trace_ref[...] = t_half[...] + t_x[...]

time: 77.8 us -> 70.5 us (0.906)
  the two profiles are of different devices: /device:TPU:19 before, /device:TPU:0 now
where the time goes in v3:
time: 70.5 us; the launch traced here: 70.2 us
  Pallas kernels  67.8 us (96%)
  local copies, waits for them, and re-layouts  2.34 us (3%)
    pallas_call x1, Pallas kernels, fast_shards(): pl.pallas_call(functools.partial(exchange_kernel, freq_count), out_shape=...  61 us
    pallas_call x1, Pallas kernels, fast_shards(): pl.pallas_call(functools.partial(inverse_kernel, factor), grid=(pieces,),...  6.83 us
    unnamed x6, local copies, waits for them, and re-layouts  2.34 us

profile of v3, /device:TPU:0, one launch (start us, length us, event | category | flops | bytes accessed | tf_op | source)
XLA Modules:
  0.0 70.2 jit_solution(15789576848022566852)
XLA Ops:
  0.0 0.0 copy-start.1
  0.0 61.0 %exchange.1 = (bf16[8,14,16,640]{3,2,1,0:T(8,128)(2,1)}, f32[8,256]{1,0:T(8,128)}) custom-call(bf16[4,64,420]{2,1,0:T(8,128)(2,1)} %constant.9.clone.table_ref, bf16[128,128]{1,0:T(8,128)(2,1)} %constant.10.clone.swap_ref, bf16[128,128]{1,0:T(8,128)(2,1)} %constant.11.clone.back_ref, f32[1,256]{1,0:T(1,128)} %bitcast.5, bf16[420,8,600]{2,1,0:T(8,128)(2,1)} %bitcast.3, ...), custom_call_target="tpu_custom_call" | custom-call | tf_op jit(solution)/shard_map/exchange/pallas_call | solution.py:450
  61.0 0.0 copy-done.1
  61.0 0.0 copy-start
  61.0 1.6 %copy-done = bf16[8,14,16,640]{3,2,1,0:T(8,128)(2,1)S(1)} copy-done((bf16[8,14,16,640]{3,2,1,0:T(8,128)(2,1)S(1)}, bf16[8,14,16,640]{3,2,1,0:T(8,128)(2,1)}, u32[]{:S(2)}) %copy-start) | copy-done | bytes 2293784
  62.7 0.0 copy-start.2
  62.7 0.7 copy-done.2
  63.4 6.8 %inverse.1 = bf16[420,8,600]{2,1,0:T(8,128)(2,1)} custom-call(bf16[8,14,16,640]{3,2,1,0:T(8,128)(2,1)S(1)} %copy-done, f32[8,256]{1,0:T(8,128)S(1)} %copy-done.2, bf16[3,140,224]{2,1,0:T(8,128)(2,1)S(1)} %copy-done.1, bf16[420,8,600]{2,1,0:T(8,128)(2,1)} %bitcast.4), custom_call_target="tpu_custom_call" | custom-call | tf_op jit(solution)/shard_map/inverse/pallas_call | solution.py:510
Async XLA Ops:
  0.0 61.0 %copy-start.1 = (bf16[3,140,224]{2,1,0:T(8,128)(2,1)S(1)}, bf16[3,140,224]{2,1,0:T(8,128)(2,1)}, u32[]{:S(2)}) copy-start(bf16[3,140,224]{2,1,0:T(8,128)(2,1)} %constant.8.clone.table_ref) | copy-start | bytes 564484
  61.0 1.6 %copy-start = (bf16[8,14,16,640]{3,2,1,0:T(8,128)(2,1)S(1)}, bf16[8,14,16,640]{3,2,1,0:T(8,128)(2,1)}, u32[]{:S(2)}) copy-start(bf16[8,14,16,640]{3,2,1,0:T(8,128)(2,1)} %get-tuple-element.7.x_ref) | copy-start | bytes 6881284
  62.7 0.7 copy-start.2
